TPU v7x, 32 devices: a whole 2x2x4 slice. The times are simulated.
32 devices in a mesh: cp: 4 (over z), tp: 8 (over y, x, core).
Axes of the slice: x: 2, y: 2, z: 4, core: 2. Of those that a mesh axis runs over, the one named last changes fastest.
Arguments:
- checkpoint: bfloat16 [2048, 8192], P('cp', 'tp'), may hold values from -6 to 6
- norm_gain: float32 [8192], replicated, may hold values from 0.1 to 1.9
- query_weight: bfloat16 [8192, 8192], P(None, 'tp'), may hold values from -4 to 4
- key_weight: bfloat16 [8192, 1024], P(None, 'tp'), may hold values from -1 to 1
- value_weight: bfloat16 [8192, 1024], P(None, 'tp'), may hold values from -0.0625 to 0.0625
- output_weight: bfloat16 [8192, 8192], P('tp'), may hold values from -0.09375 to 0.09375
- block_order: int32 [8], replicated, may hold values from 0 to 7, each once
Outputs:
- projected: bfloat16 [2048, 8192], P('cp', 'tp')
- log_normalizer: float32 [64, 2048], P('tp', 'cp')
Inputs may be any that keep to these rules, and one draw needn't show every extreme that they name: `block_order`: each of 0 to 7 once.
All inputs are finite; a program needn't handle non-finite values.
Results may differ from a plain program's by a relative error of at most 0.019.
Values may be sent and summed in bfloat16 or wider, within the bound.
No kernel may reach another device: no remote copies, remote signals or barrier semaphores. Data moves between devices by JAX's collectives and lax.ppermute only.
A program may use at most 128 MiB of HBM per device.

v0:
```python
import math
import jax
import jax.numpy as jnp
from jax import lax
from jax.sharding import PartitionSpec as P

KV_HEADS = 8
HEAD_DIM = 128
rope_base = 500000.0
norm_epsilon = 1e-05
masked_score = -1e30


def partner_2(block, axis, stride):
    count = lax.axis_size(axis)
    route = []
    for low in range(count):
        high = low | 1 << stride
        if high != low and high < count:
            route += [(low, high), (high, low)]
    return lax.ppermute(block, axis, route)


def from_behind(block, axis, distance):
    devices = range(lax.axis_size(axis))
    route = [((i - distance) % len(devices), i) for i in devices]
    return lax.ppermute(block, axis, route)


def turn_pairs(matrix, positions, first_pair):
    pair_count = matrix.shape[-1] // 2
    pair_index = (first_pair + jnp.arange(pair_count, dtype=jnp.int32)).astype(jnp.float32)
    inverse_rates = rope_base ** (-2.0 * pair_index / HEAD_DIM)
    angles = positions.astype(jnp.float32)[:, None] * inverse_rates[None, :]
    cosine = jnp.cos(angles)[:, None, :]
    sine_part = jnp.sin(angles)[:, None, :]
    paired = matrix.reshape(matrix.shape[0], matrix.shape[1], pair_count, 2)
    former = paired[..., 0]
    latter = paired[..., 1]
    turned = jnp.stack(
        [former * cosine - latter * sine_part, former * sine_part + latter * cosine], axis=-1
    )
    return turned.reshape(matrix.shape)


def shards(
    checkpoint, norm_gain, query_weight, key_weight, value_weight, output_weight, block_order
):
    tok_rows = checkpoint.shape[0]
    block_rows = tok_rows // 2
    local_heads = query_weight.shape[1] // HEAD_DIM
    key_columns = key_weight.shape[1]
    context_rank = lax.axis_index("cp")
    tensor_rank = lax.axis_index("tp")
    row_offsets = jnp.arange(block_rows, dtype=jnp.int32)
    own_blocks = lax.dynamic_slice_in_dim(block_order, 2 * context_rank, 2)
    own_positions = (own_blocks[:, None] * block_rows + row_offsets[None, :]).reshape(tok_rows)
    gathered = lax.all_gather(checkpoint, "tp", axis=1, tiled=True)
    widened = gathered.astype(jnp.float32)
    mean_square = jnp.mean(widened * widened, axis=-1, keepdims=True)
    normed = (widened * lax.rsqrt(mean_square + norm_epsilon) * norm_gain).astype(jnp.bfloat16)
    query_features = jnp.dot(normed, query_weight, preferred_element_type=jnp.float32)
    key_features = jnp.dot(normed, key_weight, preferred_element_type=jnp.float32)
    value_features = jnp.dot(normed, value_weight, preferred_element_type=jnp.float32)
    queries = turn_pairs(
        query_features.reshape(tok_rows, local_heads, HEAD_DIM), own_positions, 0
    ).astype(jnp.bfloat16)
    sharing = lax.axis_size("tp") // KV_HEADS
    part_of_head = tensor_rank % sharing
    key_part = turn_pairs(
        key_features.reshape(tok_rows, 1, key_columns),
        own_positions,
        part_of_head * (key_columns // 2),
    )
    key_part = key_part.astype(jnp.bfloat16).reshape(tok_rows, key_columns)
    value_part = value_features.astype(jnp.bfloat16)
    own_pair = jnp.stack([key_part, value_part])
    if sharing == 2:
        partner = partner_2(own_pair, "tp", 0)
        lower_first = jnp.concatenate([own_pair, partner], axis=-1)
        upper_first = jnp.concatenate([partner, own_pair], axis=-1)
        key_value = jnp.where(part_of_head == 0, lower_first, upper_first)
    else:
        key_value = own_pair
    score_scale = 1.0 / math.sqrt(HEAD_DIM)

    def absorb(running, query_slot, key_block, key_rows, value_rows):
        query_block = own_blocks[query_slot]
        top_scores, totals, weighted = running
        query_rows = queries[query_slot * block_rows : (query_slot + 1) * block_rows]
        scores = (
            jnp.einsum("qhd,kd->qhk", query_rows, key_rows, preferred_element_type=jnp.float32)
            * score_scale
        )
        query_places = query_block * block_rows + row_offsets
        key_places = key_block * block_rows + row_offsets
        allowed = (key_places[None, :] <= query_places[:, None])[:, None, :]
        scores = jnp.where(allowed, scores, masked_score)
        old_top = top_scores[query_slot]
        new_top = jnp.maximum(old_top, jnp.max(scores, axis=-1))
        weights = jnp.where(allowed, jnp.exp(scores - new_top[..., None]), 0.0)
        shrink = jnp.exp(old_top - new_top)
        new_total = totals[query_slot] * shrink + jnp.sum(weights, axis=-1)
        new_sum = weighted[query_slot] * shrink[..., None] + jnp.einsum(
            "qhk,kd->qhd",
            weights.astype(jnp.bfloat16),
            value_rows,
            preferred_element_type=jnp.float32,
        )
        return (
            top_scores.at[query_slot].set(new_top),
            totals.at[query_slot].set(new_total),
            weighted.at[query_slot].set(new_sum),
        )

    def visit_rows(running, key_value_rows, first_row):
        block_count = key_value_rows.shape[1] // block_rows

        def one_block(block_index, current):
            rows_here = lax.dynamic_slice_in_dim(
                key_value_rows, block_index * block_rows, block_rows, 1
            )
            stored = first_row // block_rows + block_index
            key_block = lax.dynamic_index_in_dim(block_order, stored, 0, keepdims=False)
            for query_slot in range(2):
                current = absorb(current, query_slot, key_block, rows_here[0], rows_here[1])
            return current

        return lax.fori_loop(0, block_count, one_block, running)

    running = (
        jnp.full((2, block_rows, local_heads), masked_score, jnp.float32),
        jnp.zeros((2, block_rows, local_heads), jnp.float32),
        jnp.zeros((2, block_rows, local_heads, HEAD_DIM), jnp.float32),
    )
    running = visit_rows(running, key_value, context_rank * tok_rows)
    context_size = lax.axis_size("cp")

    def pass_turn(turn_index, carried):
        current, travelling = carried
        travelling = from_behind(travelling, "cp", 1)
        source = (context_rank - turn_index) % context_size
        return (visit_rows(current, travelling, source * tok_rows), travelling)

    running, unused = lax.fori_loop(1, context_size, pass_turn, (running, key_value))
    top_scores, totals, weighted = running
    attended = (
        (weighted / totals[..., None])
        .astype(jnp.bfloat16)
        .reshape(tok_rows, local_heads * HEAD_DIM)
    )
    normalizer = jnp.transpose((top_scores + jnp.log(totals)).reshape(tok_rows, local_heads))
    partial_terms = jnp.dot(attended, output_weight, preferred_element_type=jnp.float32)
    projected = lax.psum_scatter(
        partial_terms.astype(jnp.bfloat16), "tp", scatter_dimension=1, tiled=True
    )
    return (projected, normalizer)


def solution(mesh):
    return jax.shard_map(
        shards,
        mesh=mesh,
        in_specs=(
            P("cp", "tp"),
            P(),
            P(None, "tp"),
            P(None, "tp"),
            P(None, "tp"),
            P("tp", None),
            P(),
        ),
        out_specs=(P("cp", "tp"), P("tp", "cp")),
        check_vma=False,
    )
```

profile of v0, /device:TPU:0, one launch (start us, length us, event | category | flops | bytes accessed | tf_op | source)
XLA Modules:
  0.0 284.2 jit_solution(17932145199853954866)
XLA Ops:
  11.1 55.8 %all-gather.2.cloned.1.call-done = bf16[512,8192]{1,0:T(8,128)(2,1)} async-done(((bf16[512,1024]{1,0:T(8,128)(2,1)}), bf16[512,8192]{1,0:T(8,128)(2,1)}) %all-gather.2.cloned.1.call-update) | async-done | bytes 8388624 | tf_op jit(solution)/shard_map/all_gather | solution.py:58
  66.9 5.1 %fusion.92 = f32[512]{0:T(512)S(1)} fusion(bf16[512,8192]{1,0:T(8,128)(2,1)} %all-gather.2.cloned.1.call-done), kind=kLoop, calls=%fused_computation.134 | loop fusion | flops 12582400 | bytes 8390656 | tf_op jit(solution)/shard_map/reduce_sum | solution.py:60
  72.0 15.5 %fusion.106 = f32[512,1024]{0,1:T(8,128)} fusion(bf16[8192,1024]{1,0:T(8,128)(2,1)} %param.39, bf16[512,8192]{1,0:T(8,128)(2,1)} %all-gather.2.cloned.1.call-done, f32[8192]{0:T(1024)S(1)} %copy-done.5, f32[512]{0:T(512)S(1)} %add_rsqrt_fusion), kind=kOutput, calls=%fused_computation.165 | convolution fusion | flops 8606711808 | bytes 27297792 | tf_op jit(solution)/shard_map/dot_general | solution.py:62
  87.6 3.5 %reshape_reshape.7 = f32[512,8,64,2]{0,3,2,1:T(2,128)} reshape(f32[512,1024]{0,1:T(8,128)} %fusion.106) | data formatting | bytes 4194304 | tf_op jit(solution)/shard_map/reshape;reshape | solution.py:37
  91.0 5.8 %fusion.109 = f32[512,128]{0,1:T(8,128)S(1)} fusion(bf16[8192,128]{1,0:T(8,128)(2,1)S(1)} %copy-done, bf16[512,8192]{1,0:T(8,128)(2,1)} %all-gather.2.cloned.1.call-done, f32[8192]{0:T(1024)S(1)} %copy-done.5, f32[512]{0:T(512)S(1)} %add_rsqrt_fusion), kind=kOutput, calls=%fused_computation.166 | convolution fusion | flops 1090519040 | bytes 10782720 | tf_op jit(solution)/shard_map/dot_general | solution.py:63
  98.4 2.9 %subtract_convert_fusion = (bf16[512,8,64,1]{0,3,2,1:T(2,128)(2,1)S(1)}, bf16[512,8,64,1]{0,3,2,1:T(2,128)(2,1)S(1)}) fusion(f32[512,8,64,2]{0,3,2,1:T(2,128)S(1)} %copy-done.2, f32[512,64]{0,1:T(8,128)S(1)} %get-tuple-element.1680, f32[512,64]{0,1:T(8,128)S(1)} %get-tuple-element.1679), kind=kLoop, calls=%fused_computation.145 | loop fusion | flops 2097152 | bytes 3407872 | tf_op jit(solution)/shard_map/convert
  101.3 2.2 pad_maximum_fusion
  103.5 1.1 copy.45
  104.7 1.2 copy.46
  105.9 6.4 %fusion.95 = bf16[1,512,128]{2,1,0:T(8,128)(2,1)S(1)} fusion(bf16[8192,128]{1,0:T(8,128)(2,1)} %param.41, bf16[512,8192]{1,0:T(8,128)(2,1)} %all-gather.2.cloned.1.call-done, f32[8192]{0:T(1024)S(1)} %copy-done.5, f32[512]{0:T(512)S(1)} %add_rsqrt_fusion), kind=kOutput, calls=%fused_computation.140 | convolution fusion | flops 1090584576 | bytes 10651648 | tf_op jit(solution)/shard_map/dot_general | solution.py:64
  113.2 11.7 %while.100 = (s32[]{:T(128)}, f32[2,256,8]{1,2,0:T(8,128)S(1)}, f32[2,256,8]{1,2,0:T(8,128)S(1)}, f32[2,256,8,128]{3,1,2,0:T(8,128)S(1)}, s32[]{:T(128)}, /*inde...) while((s32[]{:T(128)}, f32[2,256,8]{1,2,0:T(8,128)S(1)}, ...), condition=%wide.region_6.7_spmd.clone.clone, body=%wide.region_1.6_spmd.clone.clone.sunk | while | flops 551699200 | bytes 24107364 | solution.py:129
  118.1 0.9 fusion.155
  124.0 0.9 fusion.155
  124.9 65.2 %while.102 = (s32[]{:T(128)}, f32[2,256,8]{1,2,0:T(8,128)S(1)}, f32[2,256,8]{1,2,0:T(8,128)S(1)}, f32[2,256,8,128]{3,1,2,0:T(8,128)S(1)}, bf16[2,512,128]{2,1,0:...) while((s32[]{:T(128)}, f32[2,256,8]{1,2,0:T(8,128)S(1)}, ...), condition=%wide.region_14.15_spmd.clone.clone, body=%wide.region_7.14_spmd.clone.clone.sunk | while | flops 551699200 | bytes 24634376 | solution.py:145
  124.9 1.5 collective-permute-start
  126.5 9.0 %collective-permute-done = bf16[2,512,128]{2,1,0:T(8,128)(2,1)S(1)} collective-permute-done((bf16[2,512,128]{2,1,0:T(8,128)(2,1)}, bf16[2,512,128]{2,1,0:T(8,128)(2,1)S(1)}, u32[]{:S(2)}, u32[]{:S(2)}) %collective-permute-start) | collective-permute-done | bytes 262176 | tf_op jit(solution)/shard_map/while/body/eval_jaxpr/ppermute | solution.py:27
  135.5 11.4 %while.103 = (s32[]{:T(128)}, f32[2,256,8]{1,2,0:T(8,128)S(1)}, f32[2,256,8]{1,2,0:T(8,128)S(1)}, f32[2,256,8,128]{3,1,2,0:T(8,128)S(1)}, s32[]{:T(128)}, /*inde...) while((s32[]{:T(128)}, f32[2,256,8]{1,2,0:T(8,128)S(1)}, ...), condition=%wide.region_13.13_spmd.clone, body=%wide.region_8.12_spmd.clone.sunk | while | flops 551699200 | bytes 23059792 | solution.py:129
  147.6 9.6 %collective-permute-done = bf16[2,512,128]{2,1,0:T(8,128)(2,1)S(1)} collective-permute-done((bf16[2,512,128]{2,1,0:T(8,128)(2,1)}, bf16[2,512,128]{2,1,0:T(8,128)(2,1)S(1)}, u32[]{:S(2)}, u32[]{:S(2)}) %collective-permute-start) | collective-permute-done | bytes 262176 | tf_op jit(solution)/shard_map/while/body/eval_jaxpr/ppermute | solution.py:27
  157.2 11.4 %while.103 = (s32[]{:T(128)}, f32[2,256,8]{1,2,0:T(8,128)S(1)}, f32[2,256,8]{1,2,0:T(8,128)S(1)}, f32[2,256,8,128]{3,1,2,0:T(8,128)S(1)}, s32[]{:T(128)}, /*inde...) while((s32[]{:T(128)}, f32[2,256,8]{1,2,0:T(8,128)S(1)}, ...), condition=%wide.region_13.13_spmd.clone, body=%wide.region_8.12_spmd.clone.sunk | while | flops 551699200 | bytes 23059792 | solution.py:129
  169.3 8.7 %collective-permute-done = bf16[2,512,128]{2,1,0:T(8,128)(2,1)S(1)} collective-permute-done((bf16[2,512,128]{2,1,0:T(8,128)(2,1)}, bf16[2,512,128]{2,1,0:T(8,128)(2,1)S(1)}, u32[]{:S(2)}, u32[]{:S(2)}) %collective-permute-start) | collective-permute-done | bytes 262176 | tf_op jit(solution)/shard_map/while/body/eval_jaxpr/ppermute | solution.py:27
  178.0 11.4 %while.103 = (s32[]{:T(128)}, f32[2,256,8]{1,2,0:T(8,128)S(1)}, f32[2,256,8]{1,2,0:T(8,128)S(1)}, f32[2,256,8,128]{3,1,2,0:T(8,128)S(1)}, s32[]{:T(128)}, /*inde...) while((s32[]{:T(128)}, f32[2,256,8]{1,2,0:T(8,128)S(1)}, ...), condition=%wide.region_13.13_spmd.clone, body=%wide.region_8.12_spmd.clone.sunk | while | flops 551699200 | bytes 23059792 | solution.py:129
  190.2 1.0 divide_convert_fusion
  191.8 16.8 %convolution_convert_fusion = bf16[512,8192]{1,0:T(8,128)(2,1)} fusion(bf16[1024,8192]{1,0:T(8,128)(2,1)} %param.42, bf16[64,8,8,128]{3,2,1,0:T(8,128)(2,1)S(1)} %bitcast.277), kind=kOutput, calls=%fused_computation.137 | convolution fusion | flops 8594128896 | bytes 26214400 | tf_op jit(solution)/shard_map/dot_general | solution.py:153
  209.3 68.1 %reduce-scatter.2.cloned.1.call-done = bf16[512,1024]{1,0:T(8,128)(2,1)} async-done(((bf16[512,8192]{1,0:T(8,128)(2,1)}), bf16[512,1024]{1,0:T(8,128)(2,1)}) %reduce-scatter.2.cloned.1.call-update) | async-done | bytes 1048592 | tf_op jit(solution)/shard_map/reduce_scatter | solution.py:154
  (166 shorter events, 46.5 us)
Async XLA Ops:
  7.2 83.9 %copy-start = (bf16[8192,128]{1,0:T(8,128)(2,1)S(1)}, bf16[8192,128]{1,0:T(8,128)(2,1)}, u32[]{:S(2)}) copy-start(bf16[8192,128]{1,0:T(8,128)(2,1)} %param.40) | copy-start | bytes 6291460
  7.2 59.7 %all-gather.2.cloned.1.call-start = ((), (), s32[]{:S(2)}) async-start(), calls=%async_computation.1 | async-start | bytes 9437184 | tf_op jit(solution)/shard_map/all_gather | solution.py:58
  7.9 269.5 %reduce-scatter.2.cloned.1.call-start = ((), (), s32[]{:S(2)}) async-start(), calls=%async_computation.2 | async-start | bytes 9437184 | tf_op jit(solution)/shard_map/reduce_scatter | solution.py:154
  11.1 60.9 %copy-start.5 = (f32[8192]{0:T(1024)S(1)}, f32[8192]{0:T(1024)}, u32[]{:S(2)}) copy-start(f32[8192]{0:T(1024)} %param.38) | copy-start | bytes 98308
  96.8 1.6 copy-start.2
  112.2 0.9 copy-start.4
  113.2 1.6 copy-start.3
  119.1 1.6 copy-start.3
  124.9 10.5 %collective-permute-start = (bf16[2,512,128]{2,1,0:T(8,128)(2,1)}, bf16[2,512,128]{2,1,0:T(8,128)(2,1)S(1)}, u32[]{:S(2)}, u32[]{:S(2)}) collective-permute-start(bf16[2,512,128]{2,1,0:T(8,128)(2,1)} %get-tuple-element.2101), channel_id=1, source_target_pairs={{24,0},{0,8},{8,16},{16,24},{25,1},{1,9},{9,17},{17,25},{26,2},{2,... | collective-permute-start | bytes 786440 | tf_op jit(solution)/shard_map/while/body/eval_jaxpr/ppermute | solution.py:27
  147.6 9.6 %collective-permute-start = (bf16[2,512,128]{2,1,0:T(8,128)(2,1)}, bf16[2,512,128]{2,1,0:T(8,128)(2,1)S(1)}, u32[]{:S(2)}, u32[]{:S(2)}) collective-permute-start(bf16[2,512,128]{2,1,0:T(8,128)(2,1)} %get-tuple-element.2101), channel_id=1, source_target_pairs={{24,0},{0,8},{8,16},{16,24},{25,1},{1,9},{9,17},{17,25},{26,2},{2,... | collective-permute-start | bytes 786440 | tf_op jit(solution)/shard_map/while/body/eval_jaxpr/ppermute | solution.py:27
  169.3 8.7 %collective-permute-start = (bf16[2,512,128]{2,1,0:T(8,128)(2,1)}, bf16[2,512,128]{2,1,0:T(8,128)(2,1)S(1)}, u32[]{:S(2)}, u32[]{:S(2)}) collective-permute-start(bf16[2,512,128]{2,1,0:T(8,128)(2,1)} %get-tuple-element.2101), channel_id=1, source_target_pairs={{24,0},{0,8},{8,16},{16,24},{25,1},{1,9},{9,17},{17,25},{26,2},{2,... | collective-permute-start | bytes 786440 | tf_op jit(solution)/shard_map/while/body/eval_jaxpr/ppermute | solution.py:27
  208.7 68.7 %copy-start.1 = (bf16[8192,128]{1,0:T(8,128)(2,1)S(1)}, bf16[8192,128]{1,0:T(8,128)(2,1)}, u32[]{:S(2)}) copy-start(bf16[8192,128]{1,0:T(8,128)(2,1)} %param.40) | copy-start | bytes 6291460
Sparse Core Ops, SparseCore 0:
  9.9 56.9 all-gather.1
  208.8 68.5 reduce-scatter.1
where the time goes:
time: 285 us; the launch traced here: 284 us
  waiting for transfers between devices  152 us (53%)
  matrix products  66.3 us (23%)
  other arithmetic  26.9 us (9%)
  local copies, waits for them, and re-layouts  15.8 us (6%)
  between operations  15.4 us (5%)
  loops' own time  6.3 us (2%)
    reduce_scatter x1, waiting for transfers between devices, shards(): lax.psum_scatter(partial_terms.astype(jnp.bfloat16), 'tp', scatter_dimens...  68.1 us
    all_gather x1, waiting for transfers between devices, shards(): gathered = lax.all_gather(checkpoint, 'tp', axis=1, tiled=True)  55.8 us
    ppermute x3, waiting for transfers between devices, from_behind(): return lax.ppermute(block, axis, route)  27.3 us
    dot_general x1, matrix products, shards(): jnp.dot(attended, output_weight, preferred_element_type=jnp.float32)  16.8 us
    dot_general x1, matrix products, shards(): jnp.dot(normed, query_weight, preferred_element_type=jnp.float32)  15.5 us
    dot_general x16, matrix products, absorb(): jnp.einsum('qhk,kd->qhd', weights.astype(jnp.bfloat16), value_rows, prefe...  14.3 us
    reduce_sum x16, other arithmetic, absorb(): new_total = totals[query_slot] * shrink + jnp.sum(weights, axis=-1)  8.28 us
    dot_general x16, matrix products, absorb(): jnp.einsum('qhd,kd->qhk', query_rows, key_rows, preferred_element_type=jn...  7.43 us
  transfers between devices with their start and end apart: 5, of which 5 were waited for; matrix products, arithmetic and copies ran while one was open for 1% of the time, Pallas kernels for 0%

commit v1 on v0

--- a/solution.py
+++ b/solution.py
@@ -55,7 +55,20 @@
     row_offsets = jnp.arange(block_rows, dtype=jnp.int32)
     own_blocks = lax.dynamic_slice_in_dim(block_order, 2 * context_rank, 2)
     own_positions = (own_blocks[:, None] * block_rows + row_offsets[None, :]).reshape(tok_rows)
-    gathered = lax.all_gather(checkpoint, "tp", axis=1, tiled=True)
+    how_many = lax.axis_size("tp")
+    out_arr = [(no - 1, no) for no in range(1, how_many)] + [(how_many - 1, 0)]
+    inter = checkpoint
+    entries = [inter]
+    m = 0
+    while m < how_many - 1:
+        inter = lax.ppermute(inter, "tp", out_arr)
+        entries += [inter]
+        m += 1
+    gathered = jnp.roll(
+        jnp.concatenate([*reversed(entries)], axis=1),
+        (lax.axis_index("tp") + 1) * inter.shape[1],
+        axis=1,
+    )
     widened = gathered.astype(jnp.float32)
     mean_square = jnp.mean(widened * widened, axis=-1, keepdims=True)
     normed = (widened * lax.rsqrt(mean_square + norm_epsilon) * norm_gain).astype(jnp.bfloat16)

time: 285 us -> 450 us (1.58)
  local copies, waits for them, and re-layouts: 15.8 us -> 66.4 us
  waiting for transfers between devices: 152 us -> 194 us
  other arithmetic: 26.9 us -> 64.9 us
  matrix products: 66.3 us -> 96.9 us
    ppermute x0 -> x7, waiting for transfers between devices: none -> 103 us  [shards(): inter = lax.ppermute(inter, 'tp', out_arr)]
    all_gather x1 -> x0, waiting for transfers between devices: 55.8 us -> none  [shards(): gathered = lax.all_gather(checkpoint, 'tp', axis=1, tiled=True)]
    dot_general x16, matrix products: 14.3 us -> 41.4 us  [absorb(): jnp.einsum('qhk,kd->qhd', weights.astype(jnp.bfloat16), value_rows, prefe...]
    scatter x16, other arithmetic: 0.19 us -> 21 us  [absorb(): totals.at[query_slot].set(new_total)]
    unnamed x12 -> x47, local copies, waits for them, and re-layouts: 1.54 us -> 20.3 us
    slice x8, local copies, waits for them, and re-layouts: 0.56 us -> 18.2 us  [absorb(): weighted[query_slot] * shrink[..., None]]
    mul x8, other arithmetic: 2.68 us -> 12.5 us  [absorb(): weighted[query_slot] * shrink[..., None]]
    dynamic_slice x8, local copies, waits for them, and re-layouts: 4.82 us -> 9.89 us  [one_block(): key_block = lax.dynamic_index_in_dim(block_order, stored, 0, keepdims=False)]
  transfers between devices with their start and end apart: 5 -> 11, of which waited for: 5 -> 11; matrix products, arithmetic and copies ran while one was open for 1% -> 1% of each run, Pallas kernels for 0% -> 0%
where the time goes in v1:
time: 450 us; the launch traced here: 447 us
  waiting for transfers between devices  194 us (43%)
  matrix products  96.9 us (22%)
  local copies, waits for them, and re-layouts  66.4 us (15%)
  other arithmetic  64.9 us (14%)
  between operations  15.7 us (3%)
  loops' own time  5.76 us (1%)
    ppermute x7, waiting for transfers between devices, shards(): inter = lax.ppermute(inter, 'tp', out_arr)  103 us
    reduce_scatter x1, waiting for transfers between devices, shards(): lax.psum_scatter(partial_terms.astype(jnp.bfloat16), 'tp', scatter_dimens...  67.5 us
    dot_general x16, matrix products, absorb(): jnp.einsum('qhk,kd->qhd', weights.astype(jnp.bfloat16), value_rows, prefe...  41.4 us
    ppermute x3, waiting for transfers between devices, from_behind(): return lax.ppermute(block, axis, route)  23.3 us
    scatter x16, other arithmetic, absorb(): totals.at[query_slot].set(new_total)  21 us
    unnamed x47, local copies, waits for them, and re-layouts  20.3 us
    slice x8, local copies, waits for them, and re-layouts, absorb(): weighted[query_slot] * shrink[..., None]  18.2 us
    dot_general x1, matrix products, shards(): jnp.dot(attended, output_weight, preferred_element_type=jnp.float32)  16.9 us
  transfers between devices with their start and end apart: 11, of which 11 were waited for; matrix products, arithmetic and copies ran while one was open for 1% of the time, Pallas kernels for 0%

profile of v1, /device:TPU:0, one launch (start us, length us, event | category | flops | bytes accessed | tf_op | source)
XLA Modules:
  0.0 446.9 jit_solution(7735541567533220449)
XLA Ops:
  7.8 15.6 %collective-permute-done.1 = bf16[512,1024]{1,0:T(8,128)(2,1)S(1)} collective-permute-done((bf16[512,1024]{1,0:T(8,128)(2,1)}, bf16[512,1024]{1,0:T(8,128)(2,1)S(1)}, u32[]{:S(2)}, u32[]{:S(2)}) %collective-permute-start.1) | collective-permute-done | bytes 1048608 | tf_op jit(solution)/shard_map/ppermute | solution.py:64
  23.3 15.1 %collective-permute-done.2 = bf16[512,1024]{1,0:T(8,128)(2,1)S(1)} collective-permute-done((bf16[512,1024]{1,0:T(8,128)(2,1)S(1)}, bf16[512,1024]{1,0:T(8,128)(2,1)S(1)}, u32[]{:S(2)}, u32[]{:S(2)}) %collective-permute-start.2) | collective-permute-done | bytes 1048608 | tf_op jit(solution)/shard_map/ppermute | solution.py:64
  39.5 15.1 %collective-permute-done.3 = bf16[512,1024]{1,0:T(8,128)(2,1)S(1)} collective-permute-done((bf16[512,1024]{1,0:T(8,128)(2,1)S(1)}, bf16[512,1024]{1,0:T(8,128)(2,1)S(1)}, u32[]{:S(2)}, u32[]{:S(2)}) %collective-permute-start.3) | collective-permute-done | bytes 1048608 | tf_op jit(solution)/shard_map/ppermute | solution.py:64
  55.6 15.1 %collective-permute-done.4 = bf16[512,1024]{1,0:T(8,128)(2,1)S(1)} collective-permute-done((bf16[512,1024]{1,0:T(8,128)(2,1)S(1)}, bf16[512,1024]{1,0:T(8,128)(2,1)S(1)}, u32[]{:S(2)}, u32[]{:S(2)}) %collective-permute-start.4) | collective-permute-done | bytes 1048608 | tf_op jit(solution)/shard_map/ppermute | solution.py:64
  71.7 15.1 %collective-permute-done.5 = bf16[512,1024]{1,0:T(8,128)(2,1)S(1)} collective-permute-done((bf16[512,1024]{1,0:T(8,128)(2,1)S(1)}, bf16[512,1024]{1,0:T(8,128)(2,1)S(1)}, u32[]{:S(2)}, u32[]{:S(2)}) %collective-permute-start.5) | collective-permute-done | bytes 1048608 | tf_op jit(solution)/shard_map/ppermute | solution.py:64
  87.8 15.2 %collective-permute-done.6 = bf16[512,1024]{1,0:T(8,128)(2,1)} collective-permute-done((bf16[512,1024]{1,0:T(8,128)(2,1)S(1)}, bf16[512,1024]{1,0:T(8,128)(2,1)}, u32[]{:S(2)}, u32[]{:S(2)}) %collective-permute-start.6) | collective-permute-done | bytes 1048608 | tf_op jit(solution)/shard_map/ppermute | solution.py:64
  106.3 12.2 %collective-permute-done.7 = bf16[512,1024]{1,0:T(8,128)(2,1)} collective-permute-done((bf16[512,1024]{1,0:T(8,128)(2,1)}, bf16[512,1024]{1,0:T(8,128)(2,1)}, u32[]{:S(2)}, u32[]{:S(2)}) %collective-permute-start.7) | collective-permute-done | bytes 1048608 | tf_op jit(solution)/shard_map/ppermute | solution.py:64
  127.4 5.7 %copy-done.5 = bf16[512,16384]{1,0:T(8,128)(2,1)} copy-done((bf16[512,16384]{1,0:T(8,128)(2,1)}, bf16[512,16384]{1,0:T(8,128)(2,1)S(1)}, u32[]{:S(2)}) %copy-start.5) | copy-done | bytes 16777240
  134.8 15.5 %fusion.106 = f32[512,1024]{0,1:T(8,128)} fusion(bf16[8192,1024]{1,0:T(8,128)(2,1)} %param.39, f32[8192]{0:T(1024)S(1)} %copy-done.17, f32[512]{0:T(512)S(1)} %add_rsqrt_fusion, bf16[512,16384]{1,0:T(8,128)(2,1)} %copy-done.5, s32[]{:T(128)S(6)} %select_n.187), kind=kOutput, calls=%fused_computation.181 | convolution fusion | flops 8606711808 | bytes 27297796 | tf_op jit(solution)/shard_map/dot_general | solution.py:75
  150.3 3.5 reshape_reshape.7
  153.8 4.4 subtract_convert_fusion
  164.5 6.0 %fusion.109 = f32[512,128]{0,1:T(8,128)S(1)} fusion(bf16[8192,128]{1,0:T(8,128)(2,1)S(1)} %copy-done, f32[8192]{0:T(1024)S(1)} %copy-done.17, f32[512]{0:T(512)S(1)} %add_rsqrt_fusion, bf16[512,16384]{1,0:T(8,128)(2,1)} %copy-done.5, s32[]{:T(128)S(6)} %select_n.187), kind=kOutput, calls=%fused_computation.182 | convolution fusion | flops 1090519040 | bytes 10782724 | tf_op jit(solution)/shard_map/dot_general | solution.py:76
  171.8 6.4 %fusion.95 = bf16[1,512,128]{2,1,0:T(8,128)(2,1)S(1)} fusion(bf16[8192,128]{1,0:T(8,128)(2,1)} %param.41, f32[8192]{0:T(1024)S(1)} %copy-done.17, f32[512]{0:T(512)S(1)} %add_rsqrt_fusion, bf16[512,16384]{1,0:T(8,128)(2,1)} %copy-done.5, s32[]{:T(128)S(6)} %select_n.187), kind=kOutput, calls=%fused_computation.140 | convolution fusion | flops 1090584576 | bytes 10651652 | tf_op jit(solution)/shard_map/dot_general | solution.py:77
  181.1 36.1 %while.100 = (s32[]{:T(128)}, f32[2,256,8]{1,2,0:T(8,128)S(1)}, f32[2,256,8]{1,2,0:T(8,128)}, f32[2,256,8,128]{3,1,2,0:T(8,128)}, s32[]{:T(128)}, /*index=5*/s32...) while((s32[]{:T(128)}, f32[2,256,8]{1,2,0:T(8,128)S(1)}, ...), condition=%wide.region_6.7_spmd.clone.clone, body=%wide.region_1.6_spmd.clone.clone.sunk | while | flops 551699200 | bytes 23058752 | solution.py:142
  186.7 3.1 fusion.153
  217.2 134.3 %while.102 = (s32[]{:T(128)}, f32[2,256,8]{1,2,0:T(8,128)S(1)}, f32[2,256,8]{1,2,0:T(8,128)}, f32[2,256,8,128]{3,1,2,0:T(8,128)}, bf16[2,512,128]{2,1,0:T(8,128)...) while((s32[]{:T(128)}, f32[2,256,8]{1,2,0:T(8,128)S(1)}, ...), condition=%wide.region_14.15_spmd.clone.clone, body=%wide.region_7.0_spmd.clone.clone.sunk | while | flops 551699200 | bytes 24732756 | solution.py:158
  219.5 6.6 %collective-permute-done = bf16[2,512,128]{2,1,0:T(8,128)(2,1)S(1)} collective-permute-done((bf16[2,512,128]{2,1,0:T(8,128)(2,1)}, bf16[2,512,128]{2,1,0:T(8,128)(2,1)S(1)}, u32[]{:S(2)}, u32[]{:S(2)}) %collective-permute-start) | collective-permute-done | bytes 262176 | tf_op jit(solution)/shard_map/while/body/eval_jaxpr/ppermute | solution.py:27
  226.6 35.0 %while.103 = (s32[]{:T(128)}, f32[2,256,8]{1,2,0:T(8,128)S(1)}, f32[2,256,8]{1,2,0:T(8,128)}, f32[2,256,8,128]{3,1,2,0:T(8,128)}, s32[]{:T(128)}, /*index=5*/s32...) while((s32[]{:T(128)}, f32[2,256,8]{1,2,0:T(8,128)S(1)}, ...), condition=%wide.region_13.13_spmd.clone, body=%wide.region_8.12_spmd.clone.sunk | while | flops 551699200 | bytes 23158172 | solution.py:142
  262.3 8.4 %collective-permute-done = bf16[2,512,128]{2,1,0:T(8,128)(2,1)S(1)} collective-permute-done((bf16[2,512,128]{2,1,0:T(8,128)(2,1)}, bf16[2,512,128]{2,1,0:T(8,128)(2,1)S(1)}, u32[]{:S(2)}, u32[]{:S(2)}) %collective-permute-start) | collective-permute-done | bytes 262176 | tf_op jit(solution)/shard_map/while/body/eval_jaxpr/ppermute | solution.py:27
  271.2 35.0 %while.103 = (s32[]{:T(128)}, f32[2,256,8]{1,2,0:T(8,128)S(1)}, f32[2,256,8]{1,2,0:T(8,128)}, f32[2,256,8,128]{3,1,2,0:T(8,128)}, s32[]{:T(128)}, /*index=5*/s32...) while((s32[]{:T(128)}, f32[2,256,8]{1,2,0:T(8,128)S(1)}, ...), condition=%wide.region_13.13_spmd.clone, body=%wide.region_8.12_spmd.clone.sunk | while | flops 551699200 | bytes 23158172 | solution.py:142
  306.9 8.4 %collective-permute-done = bf16[2,512,128]{2,1,0:T(8,128)(2,1)S(1)} collective-permute-done((bf16[2,512,128]{2,1,0:T(8,128)(2,1)}, bf16[2,512,128]{2,1,0:T(8,128)(2,1)S(1)}, u32[]{:S(2)}, u32[]{:S(2)}) %collective-permute-start) | collective-permute-done | bytes 262176 | tf_op jit(solution)/shard_map/while/body/eval_jaxpr/ppermute | solution.py:27
  315.8 35.0 %while.103 = (s32[]{:T(128)}, f32[2,256,8]{1,2,0:T(8,128)S(1)}, f32[2,256,8]{1,2,0:T(8,128)}, f32[2,256,8,128]{3,1,2,0:T(8,128)}, s32[]{:T(128)}, /*index=5*/s32...) while((s32[]{:T(128)}, f32[2,256,8]{1,2,0:T(8,128)S(1)}, ...), condition=%wide.region_13.13_spmd.clone, body=%wide.region_8.12_spmd.clone.sunk | while | flops 551699200 | bytes 23158172 | solution.py:142
  354.1 16.9 %convolution_convert_fusion = bf16[512,8192]{1,0:T(8,128)(2,1)} fusion(bf16[1024,8192]{1,0:T(8,128)(2,1)} %param.42, bf16[64,8,8,128]{3,2,1,0:T(8,128)(2,1)S(1)} %bitcast.277), kind=kOutput, calls=%fused_computation.137 | convolution fusion | flops 8594128896 | bytes 26214400 | tf_op jit(solution)/shard_map/dot_general | solution.py:166
  372.5 67.5 %reduce-scatter.2.cloned.1.call-done = bf16[512,1024]{1,0:T(8,128)(2,1)} async-done(((bf16[512,8192]{1,0:T(8,128)(2,1)}), bf16[512,1024]{1,0:T(8,128)(2,1)}) %reduce-scatter.2.cloned.1.call-update) | async-done | bytes 1048592 | tf_op jit(solution)/shard_map/reduce_scatter | solution.py:167
  (245 shorter events, 169.7 us)
Async XLA Ops:
  7.2 157.3 %copy-start = (bf16[8192,128]{1,0:T(8,128)(2,1)S(1)}, bf16[8192,128]{1,0:T(8,128)(2,1)}, u32[]{:S(2)}) copy-start(bf16[8192,128]{1,0:T(8,128)(2,1)} %param.40) | copy-start | bytes 6291460
  7.2 432.8 %reduce-scatter.2.cloned.1.call-start = ((), (), s32[]{:S(2)}) async-start(), calls=%async_computation.1 | async-start | bytes 9437184 | tf_op jit(solution)/shard_map/reduce_scatter | solution.py:167
  7.2 16.1 %collective-permute-start.1 = (bf16[512,1024]{1,0:T(8,128)(2,1)}, bf16[512,1024]{1,0:T(8,128)(2,1)S(1)}, u32[]{:S(2)}, u32[]{:S(2)}) collective-permute-start(bf16[512,1024]{1,0:T(8,128)(2,1)} %param.37), channel_id=1, source_target_pairs={{0,1},{1,2},{2,3},{3,4},{4,5},{5,6},{6,7},{7,0},{8,9},{9,10},{10,1... | collective-permute-start | bytes 3145736 | tf_op jit(solution)/shard_map/ppermute | solution.py:64
  23.3 97.9 %copy-start.7 = (bf16[512,1024]{1,0:T(8,128)(2,1)}, bf16[512,1024]{1,0:T(8,128)(2,1)S(1)}, u32[]{:S(2)}) copy-start(bf16[512,1024]{1,0:T(8,128)(2,1)S(1)} %collective-permute-done.1) | copy-start | bytes 3145732
  23.3 15.1 %collective-permute-start.2 = (bf16[512,1024]{1,0:T(8,128)(2,1)S(1)}, bf16[512,1024]{1,0:T(8,128)(2,1)S(1)}, u32[]{:S(2)}, u32[]{:S(2)}) collective-permute-start(bf16[512,1024]{1,0:T(8,128)(2,1)S(1)} %collective-permute-done.1), channel_id=1, source_target_pairs={{0,1},{1,2},{2,3},{3,4},{4,5},{5,6},{6,7},{7,0},{8,9},{9,10},{10,1... | collective-permute-start | bytes 3145736 | tf_op jit(solution)/shard_map/ppermute | solution.py:64
  39.5 15.1 %collective-permute-start.3 = (bf16[512,1024]{1,0:T(8,128)(2,1)S(1)}, bf16[512,1024]{1,0:T(8,128)(2,1)S(1)}, u32[]{:S(2)}, u32[]{:S(2)}) collective-permute-start(bf16[512,1024]{1,0:T(8,128)(2,1)S(1)} %collective-permute-done.2), channel_id=1, source_target_pairs={{0,1},{1,2},{2,3},{3,4},{4,5},{5,6},{6,7},{7,0},{8,9},{9,10},{10,1... | collective-permute-start | bytes 3145736 | tf_op jit(solution)/shard_map/ppermute | solution.py:64
  55.6 15.1 %collective-permute-start.4 = (bf16[512,1024]{1,0:T(8,128)(2,1)S(1)}, bf16[512,1024]{1,0:T(8,128)(2,1)S(1)}, u32[]{:S(2)}, u32[]{:S(2)}) collective-permute-start(bf16[512,1024]{1,0:T(8,128)(2,1)S(1)} %collective-permute-done.3), channel_id=1, source_target_pairs={{0,1},{1,2},{2,3},{3,4},{4,5},{5,6},{6,7},{7,0},{8,9},{9,10},{10,1... | collective-permute-start | bytes 3145736 | tf_op jit(solution)/shard_map/ppermute | solution.py:64
  71.7 15.1 %collective-permute-start.5 = (bf16[512,1024]{1,0:T(8,128)(2,1)S(1)}, bf16[512,1024]{1,0:T(8,128)(2,1)S(1)}, u32[]{:S(2)}, u32[]{:S(2)}) collective-permute-start(bf16[512,1024]{1,0:T(8,128)(2,1)S(1)} %collective-permute-done.4), channel_id=1, source_target_pairs={{0,1},{1,2},{2,3},{3,4},{4,5},{5,6},{6,7},{7,0},{8,9},{9,10},{10,1... | collective-permute-start | bytes 3145736 | tf_op jit(solution)/shard_map/ppermute | solution.py:64
  87.8 15.2 %collective-permute-start.6 = (bf16[512,1024]{1,0:T(8,128)(2,1)S(1)}, bf16[512,1024]{1,0:T(8,128)(2,1)}, u32[]{:S(2)}, u32[]{:S(2)}) collective-permute-start(bf16[512,1024]{1,0:T(8,128)(2,1)S(1)} %collective-permute-done.5), channel_id=1, source_target_pairs={{0,1},{1,2},{2,3},{3,4},{4,5},{5,6},{6,7},{7,0},{8,9},{9,10},{10,1... | collective-permute-start | bytes 3145736 | tf_op jit(solution)/shard_map/ppermute | solution.py:64
  103.0 15.4 %collective-permute-start.7 = (bf16[512,1024]{1,0:T(8,128)(2,1)}, bf16[512,1024]{1,0:T(8,128)(2,1)}, u32[]{:S(2)}, u32[]{:S(2)}) collective-permute-start(bf16[512,1024]{1,0:T(8,128)(2,1)} %collective-permute-done.6), channel_id=1, source_target_pairs={{0,1},{1,2},{2,3},{3,4},{4,5},{5,6},{6,7},{7,0},{8,9},{9,10},{10,1... | collective-permute-start | bytes 3145736 | tf_op jit(solution)/shard_map/ppermute | solution.py:64
  106.3 14.9 %copy-start.16 = (bf16[512,1024]{1,0:T(8,128)(2,1)S(1)}, bf16[512,1024]{1,0:T(8,128)(2,1)}, u32[]{:S(2)}) copy-start(bf16[512,1024]{1,0:T(8,128)(2,1)} %copy-done.15) | copy-start | bytes 3145732
  119.8 1.5 copy-start.14
  127.4 5.7 %copy-start.5 = (bf16[512,16384]{1,0:T(8,128)(2,1)}, bf16[512,16384]{1,0:T(8,128)(2,1)S(1)}, u32[]{:S(2)}) copy-start(bf16[512,16384]{1,0:T(8,128)(2,1)S(1)} %constant_dynamic-update-slice_fusion) | copy-start | bytes 50331652
  133.1 1.7 copy-start.17
  217.2 8.9 %collective-permute-start = (bf16[2,512,128]{2,1,0:T(8,128)(2,1)}, bf16[2,512,128]{2,1,0:T(8,128)(2,1)S(1)}, u32[]{:S(2)}, u32[]{:S(2)}) collective-permute-start(bf16[2,512,128]{2,1,0:T(8,128)(2,1)} %get-tuple-element.2101), channel_id=1, source_target_pairs={{24,0},{0,8},{8,16},{16,24},{25,1},{1,9},{9,17},{17,25},{26,2},{2,... | collective-permute-start | bytes 786440 | tf_op jit(solution)/shard_map/while/body/eval_jaxpr/ppermute | solution.py:27
  233.3 3.1 copy-start.4
  250.8 3.1 copy-start.4
  262.3 8.4 %collective-permute-start = (bf16[2,512,128]{2,1,0:T(8,128)(2,1)}, bf16[2,512,128]{2,1,0:T(8,128)(2,1)S(1)}, u32[]{:S(2)}, u32[]{:S(2)}) collective-permute-start(bf16[2,512,128]{2,1,0:T(8,128)(2,1)} %get-tuple-element.2101), channel_id=1, source_target_pairs={{24,0},{0,8},{8,16},{16,24},{25,1},{1,9},{9,17},{17,25},{26,2},{2,... | collective-permute-start | bytes 786440 | tf_op jit(solution)/shard_map/while/body/eval_jaxpr/ppermute | solution.py:27
  277.9 3.1 copy-start.4
  295.3 3.1 copy-start.4
  306.9 8.4 %collective-permute-start = (bf16[2,512,128]{2,1,0:T(8,128)(2,1)}, bf16[2,512,128]{2,1,0:T(8,128)(2,1)S(1)}, u32[]{:S(2)}, u32[]{:S(2)}) collective-permute-start(bf16[2,512,128]{2,1,0:T(8,128)(2,1)} %get-tuple-element.2101), channel_id=1, source_target_pairs={{24,0},{0,8},{8,16},{16,24},{25,1},{1,9},{9,17},{17,25},{26,2},{2,... | collective-permute-start | bytes 786440 | tf_op jit(solution)/shard_map/while/body/eval_jaxpr/ppermute | solution.py:27
  322.5 3.1 copy-start.4
  339.9 3.1 copy-start.4
  371.0 69.0 %copy-start.1 = (bf16[8192,128]{1,0:T(8,128)(2,1)S(1)}, bf16[8192,128]{1,0:T(8,128)(2,1)}, u32[]{:S(2)}) copy-start(bf16[8192,128]{1,0:T(8,128)(2,1)} %param.40) | copy-start | bytes 6291460
  (20 other events, 17.0 us)
Sparse Core Ops, SparseCore 0:
  371.1 68.8 reduce-scatter.1
